TPU v7x, 256 devices: a whole 4x4x8 slice. The times are simulated.
256 devices in a mesh: slab: 8 (over z_lo, x), grp: 32 (over y, z_hi, core).
Axes of the slice: x: 4, y: 4, z: 8 (z_hi: 4, z_lo: 2; z = z_hi * 2 + z_lo), core: 2. Of those that a mesh axis runs over, the one named last changes fastest.
Arguments:
- blocks: bfloat16 [1024, 9, 256, 256], P(('slab', 'grp')), may hold values from -0.75 to 0.75
- diag_shift: float32 [262144], P(('slab', 'grp')), may hold values from 1 to 16
- offsets: int32 [1024, 2], P(('slab', 'grp')), may hold values from 0 to 4
Outputs:
- factors: bfloat16 [1024, 9, 256, 256], P(('slab', 'grp'))
Inputs may be any that keep to these rules, and one draw needn't show every extreme that they name: offsets[i, 0] bounds from above the pattern's blocks left of the diagonal block of block row i and offsets[i, 1] those right of it; blocks that would lie outside the matrix are not in the pattern.
All inputs are finite; a program needn't handle non-finite values.
Results may differ from a plain program's by a relative error of at most 0.001.
Values may be sent and summed in bfloat16 or wider, within the bound.
A program may use at most 256 MiB of HBM per device.

v0:
```python
import functools

import jax
import jax.numpy as jnp
from jax import lax
from jax.experimental import pallas as pl
from jax.experimental.pallas import tpu as pltpu
from jax.sharding import PartitionSpec as P

MESH = pl.DeviceIdType.MESH
F32 = jnp.float32
BF16 = jnp.bfloat16
BW = 4
LANES = 128


def mm(lhs, rhs):
    lhs = lhs[0] if len(lhs) == 1 else jnp.concatenate(lhs, axis=1)
    rhs = rhs[0] if len(rhs) == 1 else jnp.concatenate(rhs, axis=0)
    return jnp.dot(lhs, rhs, preferred_element_type=F32)


def kernel(
    n_slab, n_grp,
    blocks, shift, offs, out,
    w0, l0, w1, l1, wo, lo,
    base, msg, above, below, reach, sc, rs, rd,
    in_sem, out_sem, m_send, m_recv, x_send, x_recv, y_send, y_recv, q_send, q_recv,
):
    rows, _, size, _ = blocks.shape
    half = size // 2
    slab, grp = lax.axis_index("slab"), lax.axis_index("grp")
    flat = slab * n_grp + grp
    total = n_slab * n_grp
    has_prev, has_next = flat > 0, flat < total - 1
    after, before = jnp.minimum(flat + 1, total - 1), jnp.maximum(flat - 1, 0)
    nxt = (after // n_grp, after % n_grp)
    prv = (before // n_grp, before % n_grp)
    inside = grp < n_grp - 1
    edge_out = jnp.logical_and(has_next, grp == n_grp - 1)
    edge_in = jnp.logical_and(has_prev, grp == 0)

    def remote(src, dst, send, recv, where_to):
        return pltpu.make_async_remote_copy(
            src_ref=src, dst_ref=dst, send_sem=send, recv_sem=recv, device_id=where_to, device_id_type=MESH
        )

    loads = [
        pltpu.make_async_copy(blocks.at[:, BW], w0.at[pl.ds(BW, rows), 0], in_sem.at[0]),
        pltpu.make_async_copy(blocks.at[:, pl.ds(BW + 1, BW)], w0.at[pl.ds(BW, rows), pl.ds(1, BW)], in_sem.at[1]),
        pltpu.make_async_copy(blocks.at[:, pl.ds(0, BW)], l0, in_sem.at[2]),
    ]
    for load in loads:
        load.start()

    barrier = pltpu.get_barrier_semaphore()

    @pl.when(has_next)
    def _():
        pl.semaphore_signal(barrier, inc=1, device_id=nxt, device_id_type=MESH)

    @pl.when(has_prev)
    def _():
        pl.semaphore_signal(barrier, inc=1, device_id=prv, device_id_type=MESH)

    pl.semaphore_wait(barrier, has_next.astype(jnp.int32) + has_prev.astype(jnp.int32))

    def x_parts(source):
        parts = []
        for r in range(rows - 1, -1, -1):
            first, count = BW - r, r + 1
            parts.append(remote(source(r, first, count), w0.at[r, pl.ds(first, count)], x_send.at[r], x_recv.at[r], nxt))
        for r in range(rows - 1, -1, -1):
            count = BW - r
            at = rows + r
            parts.append(remote(source(r, 0, count), w0.at[r, pl.ds(0, count)], x_send.at[at], x_recv.at[at], nxt))
        return parts

    def y_part(row_ref, r, kind):
        at = r * 4 + kind
        dst = w1.at[r]
        if kind == 0:
            cut = (pl.ds(BW - r, r),)
        elif kind == 1:
            cut = (pl.ds(1, BW - 1 - r),)
        elif kind == 2:
            cut = (0, pl.ds(0, half))
        else:
            cut = (0, pl.ds(half, half), pl.ds(half, half))
        return remote(row_ref.at[cut], dst.at[cut], y_send.at[at], y_recv.at[at], nxt)

    def y_parts(source):
        order = [(r, 0) for r in range(rows - 1, 0, -1)]
        for r in range(rows - 1, -1, -1):
            order += [(r, 1)] * (r < rows - 1) + [(r, 2), (r, 3)]
        return [y_part(source(r), r, kind) for r, kind in order]

    from_input = x_parts(lambda r, first, count: blocks.at[r, pl.ds(BW + first, count)])
    from_first = x_parts(lambda r, first, count: w1.at[BW + r, pl.ds(first, count)])
    q_copy = remote(blocks.at[:, 2 * BW], base, q_send, q_recv, nxt)

    @pl.when(inside)
    def _():
        for part in from_input:
            part.start()

    @pl.when(edge_out)
    def _():
        q_copy.start()

    @pl.when(jnp.logical_not(has_prev))
    def _():
        above[...] = jnp.zeros_like(above)

        def clear(i, c):
            a, t = i // (BW + 1), i % (BW + 1)
            w0[a, t] = jnp.zeros((size, size), BF16)
            w1[a, t] = jnp.zeros((size, size), BF16)
            return c

        lax.fori_loop(0, BW * (BW + 1), clear, 0)

    @pl.when(jnp.logical_not(has_next))
    def _():
        below[...] = jnp.zeros_like(below)

    row_id = lax.broadcasted_iota(jnp.int32, (size, size), 0)
    col_id = lax.broadcasted_iota(jnp.int32, (size, size), 1)
    eye = row_id == col_id

    def diagonal(block):
        return jnp.sum(jnp.where(eye, block.astype(F32), 0.0), axis=0, keepdims=True)

    loads[0].wait()
    for r in range(rows):
        msg[pl.ds(r, 1), :] = shift[pl.ds(r, 1), :] + diagonal(w0[BW + r, 0])
        at = flat * rows + r
        up = jnp.minimum(offs[r, 1], total * rows - 1 - at)
        down = jnp.minimum(offs[r, 0], at)
        msg[pl.ds(rows + r, 1), :] = jnp.broadcast_to(up.astype(F32), (1, size))
        reach[pl.ds(r, 1), :] = jnp.broadcast_to(down.astype(F32), (1, size))
    to_next = remote(msg, above, m_send.at[0], m_recv.at[0], nxt)
    to_prev = remote(msg, below, m_send.at[1], m_recv.at[1], prv)

    @pl.when(has_next)
    def _():
        to_next.start()

    @pl.when(has_prev)
    def _():
        to_prev.start()

    loads[1].wait()
    loads[2].wait()

    @pl.when(has_prev)
    def _():
        to_next.wait_recv()

    @pl.when(has_next)
    def _():
        to_prev.wait_recv()

    def scale_of(values):
        positive = values > 0
        return jnp.where(positive, 1.0 / jnp.sqrt(jnp.where(positive, values, 1.0)), 0.0)

    sc[pl.ds(0, rows), :] = scale_of(above[pl.ds(0, rows), :])
    sc[pl.ds(rows, rows), :] = scale_of(msg[pl.ds(0, rows), :])
    sc[pl.ds(2 * rows, rows), :] = scale_of(below[pl.ds(0, rows), :])

    def spread(j, c):
        column = jnp.sum(jnp.where(eye, jnp.broadcast_to(sc[pl.ds(j, 1), :], (size, size)), 0.0), axis=1, keepdims=True)
        rs[j] = jnp.broadcast_to(column, (size, LANES))
        return c

    lax.fori_loop(0, 2 * rows, spread, 0)

    def scaled(block, j, column, keep):
        row_scale = jnp.concatenate([rs[j]] * (size // LANES), axis=1)
        value = block.astype(F32) * row_scale * sc[pl.ds(column, 1), :]
        return jnp.where(jnp.broadcast_to(keep, (size, size)), value, 0.0).astype(BF16)

    def scaled_diag(block, j, values):
        row_scale = jnp.concatenate([rs[j]] * (size // LANES), axis=1)
        full = jnp.where(eye, jnp.broadcast_to(values, (size, size)), block.astype(F32))
        return (full * row_scale * sc[pl.ds(j, 1), :]).astype(BF16)

    def own_upper(i, c):
        r, t = i // BW, 1 + i % BW
        keep = msg[pl.ds(rows + r, 1), :] >= t.astype(F32)
        w0[BW + r, t] = scaled(w0[BW + r, t], BW + r, BW + r + t, keep)
        return c

    def own_lower(i, c):
        r, k = i // BW, i % BW
        keep = reach[pl.ds(r, 1), :] >= (BW - k).astype(F32)
        l0[r, k] = scaled(l0[r, k], BW + r, r + k, keep)
        return c

    def own_diag(r, c):
        w0[BW + r, 0] = scaled_diag(w0[BW + r, 0], BW + r, msg[pl.ds(r, 1), :])
        return c

    lax.fori_loop(0, rows, own_diag, 0)
    lax.fori_loop(0, rows * BW, own_upper, 0)
    lax.fori_loop(0, rows * BW, own_lower, 0)

    def above_upper(a):
        def step(t, c):
            keep = above[pl.ds(rows + a, 1), :] >= t.astype(F32)
            w0[a, t] = scaled(w0[a, t], a, a + t, keep)
            return c

        return step

    strict_up, strict_low = col_id > row_id, row_id > col_id

    def keep_if(mask, block):
        return jnp.where(mask, block.astype(F32), 0.0).astype(BF16)

    def upper_row(r, w, l, w_new, new_row):
        own = w[BW + r, 0]
        low = keep_if(strict_low, own)
        pivot = 1.0 / diagonal(own)
        rd[pl.ds(BW + r, 1), :] = pivot
        for t in range(BW + 1):
            lhs, rhs = [low], [keep_if(strict_up, own) if t == 0 else w[BW + r, t]]
            for m in range(1, BW + 1 - t):
                lhs.append(l[r, BW - m])
                rhs.append(w[BW + r - m, t + m])
            value = w0[BW + r, t].astype(F32) - mm(lhs, rhs)
            if t == 0:
                value = jnp.where(strict_low, value * pivot, value)
            else:
                keep = msg[pl.ds(rows + r, 1), :] >= float(t)
                value = jnp.where(jnp.broadcast_to(keep, (size, size)), value, 0.0)
            w_new[new_row, t] = value.astype(BF16)

    def lower_row(r, w, l, l_new):
        for k in range(BW):
            m = BW - k
            lhs, rhs = [l[r, k]], [keep_if(strict_up, w[BW + r - m, 0])]
            for back in range(m + 1, BW + 1):
                lhs.append(l[r, BW - back])
                rhs.append(w[BW + r - back, back - m])
            value = (l0[r, k].astype(F32) - mm(lhs, rhs)) * rd[pl.ds(BW + r - m, 1), :]
            keep = reach[pl.ds(r, 1), :] >= float(m)
            l_new[r, k] = jnp.where(jnp.broadcast_to(keep, (size, size)), value, 0.0).astype(BF16)

    def arrive(r, pieces):
        for c in range(rows):

            @pl.when(jnp.logical_and(has_prev, r == c))
            def _():
                for piece in pieces[c]:
                    piece.wait_recv()

    x_first = [[p] for p in reversed(from_input[:rows])]
    x_rest = [[p] for p in reversed(from_input[rows:])]
    y_first = [[y_part(w1.at[BW + r], r, 0)] if r else [] for r in range(rows)]
    y_rest = [
        [y_part(w1.at[BW + r], r, kind) for kind in ((1, 2, 3) if r < rows - 1 else (2, 3))] for r in range(rows)
    ]

    @pl.when(edge_in)
    def _():
        q_copy.wait_recv()

    def upper_1(i, c):
        r = rows - 1 - i
        arrive(r, x_first)

        @pl.when(grp > 0)
        def _():
            lax.fori_loop(BW - r, BW + 1, above_upper(r), 0)
            base[r] = w0[r, BW]

        @pl.when(grp == 0)
        def _():
            keep = above[pl.ds(rows + r, 1), :] >= float(BW)
            base[r] = scaled(base[r], r, r + BW, keep)

        upper_row(r, w0, l0, w1, BW + r)
        return c

    @pl.when(jnp.logical_not(has_prev))
    def _():
        def clear(a, c):
            base[a] = jnp.zeros((size, size), BF16)
            return c

        lax.fori_loop(0, rows, clear, 0)

    lax.fori_loop(0, rows, upper_1, 0)

    @pl.when(inside)
    def _():
        for part in y_parts(lambda r: w1.at[BW + r]):
            part.start()

    @pl.when(edge_out)
    def _():
        for part in from_first:
            part.start()

    def lower_1(i, c):
        r = rows - 1 - i
        arrive(r, x_rest)

        @pl.when(grp > 0)
        def _():
            w0[r, 0] = scaled_diag(w0[r, 0], r, above[pl.ds(r, 1), :])
            lax.fori_loop(1, BW - r, above_upper(r), 0)

        rd[pl.ds(r, 1), :] = 1.0 / diagonal(w0[r, 0])
        lower_row(r, w0, l0, l1)
        return c

    lax.fori_loop(0, rows, lower_1, 0)

    outs_up = [pltpu.make_async_copy(wo.at[r], out.at[r, pl.ds(BW, BW + 1)], out_sem.at[r]) for r in range(rows)]
    outs_low = [pltpu.make_async_copy(lo.at[r], out.at[r, pl.ds(0, BW)], out_sem.at[rows + r]) for r in range(rows)]

    def leave(r, copies):
        for c in range(rows):

            @pl.when(r == c)
            def _():
                copies[c].start()

    def upper_2(i, c):
        r = rows - 1 - i
        arrive(r, y_first)
        keep = above[pl.ds(rows + r, 1), :] >= float(BW)
        value = base[r].astype(F32) - mm([keep_if(strict_low, w0[r, 0])], [w0[r, BW]])
        w1[r, BW] = jnp.where(jnp.broadcast_to(keep, (size, size)), value, 0.0).astype(BF16)
        upper_row(r, w1, l1, wo, r)
        return c

    lax.fori_loop(0, rows, upper_2, 0)

    @pl.when(edge_out)
    def _():
        for part in y_parts(lambda r: wo.at[r]):
            part.start()

    for copy in outs_up:
        copy.start()

    def lower_2(i, c):
        r = rows - 1 - i
        arrive(r, y_rest)
        rd[pl.ds(r, 1), :] = 1.0 / diagonal(w1[r, 0])
        lower_row(r, w1, l1, lo)
        leave(r, outs_low)
        return c

    lax.fori_loop(0, rows, lower_2, 0)

    @pl.when(has_next)
    def _():
        for part in from_input + y_parts(lambda r: w1.at[BW + r]) + [to_next]:
            part.wait_send()

    @pl.when(edge_out)
    def _():
        q_copy.wait_send()

    @pl.when(has_prev)
    def _():
        to_prev.wait_send()

    for copy in outs_up + outs_low:
        copy.wait()


def per_device(n_slab, n_grp, blocks, diag_shift, offsets):
    rows, band, size, _ = blocks.shape
    block = (size, size)
    call = pl.pallas_call(
        functools.partial(kernel, n_slab, n_grp),
        out_shape=jax.ShapeDtypeStruct(blocks.shape, BF16),
        in_specs=[
            pl.BlockSpec(memory_space=pl.ANY),
            pl.BlockSpec(memory_space=pltpu.VMEM),
            pl.BlockSpec(memory_space=pltpu.SMEM),
        ],
        out_specs=pl.BlockSpec(memory_space=pl.ANY),
        scratch_shapes=[
            pltpu.VMEM((2 * rows, BW + 1) + block, BF16),
            pltpu.VMEM((rows, BW) + block, BF16),
            pltpu.VMEM((2 * rows, BW + 1) + block, BF16),
            pltpu.VMEM((rows, BW) + block, BF16),
            pltpu.VMEM((rows, BW + 1) + block, BF16),
            pltpu.VMEM((rows, BW) + block, BF16),
            pltpu.VMEM((rows,) + block, BF16),
            pltpu.VMEM((2 * rows, size), F32),
            pltpu.VMEM((2 * rows, size), F32),
            pltpu.VMEM((2 * rows, size), F32),
            pltpu.VMEM((2 * rows, size), F32),
            pltpu.VMEM((4 * rows, size), F32),
            pltpu.VMEM((2 * rows, size, LANES), F32),
            pltpu.VMEM((2 * rows, size), F32),
            pltpu.SemaphoreType.DMA((3,)),
            pltpu.SemaphoreType.DMA((2 * rows,)),
            pltpu.SemaphoreType.DMA((2,)),
            pltpu.SemaphoreType.DMA((2,)),
            pltpu.SemaphoreType.DMA((2 * rows,)),
            pltpu.SemaphoreType.DMA((2 * rows,)),
            pltpu.SemaphoreType.DMA((4 * rows,)),
            pltpu.SemaphoreType.DMA((4 * rows,)),
            pltpu.SemaphoreType.DMA,
            pltpu.SemaphoreType.DMA,
        ],
        compiler_params=pltpu.CompilerParams(
            collective_id=0, has_side_effects=True, vmem_limit_bytes=60 * 1024 * 1024
        ),
        name="sweeps",
    )
    return call(blocks, diag_shift.reshape(rows, size), offsets)


def solution(mesh):
    return jax.shard_map(
        functools.partial(per_device, mesh.shape["slab"], mesh.shape["grp"]),
        mesh=mesh,
        in_specs=(
            P(("slab", "grp"), None, None, None),
            P(("slab", "grp")),
            P(("slab", "grp"), None),
        ),
        out_specs=P(("slab", "grp"), None, None, None),
        check_vma=False,
    )
```

profile of v0, /device:TPU:38, one launch (start us, length us, event | category | flops | bytes accessed | tf_op | source)
XLA Modules:
  0.0 135.1 jit_solution(1252071950286152647)
XLA Ops:
  0.0 1.3 copy.4.offs
  1.3 1.3 reshape.3.shift
  2.6 127.4 %sweeps.1 = bf16[4,9,256,256]{3,2,1,0:T(8,128)(2,1)} custom-call(bf16[4,9,256,256]{3,2,1,0:T(8,128)(2,1)} %blocks.1, f32[4,256]{1,0:T(4,128)} %reshape.3.shift, s32[4,2]{1,0:T(4,128)} %copy.4.offs), custom_call_target="tpu_custom_call" | custom-call | tf_op jit(solution)/shard_map/sweeps/pallas_call | solution.py:421
  130.0 5.0 %copy.6 = bf16[4,9,256,256]{3,2,1,0:T(8,128)(2,1)} copy(bf16[4,9,256,256]{3,2,1,0:T(8,128)(2,1)} %sweeps.1) | data formatting | bytes 9437184
where the time goes:
time: 135 us
  Pallas kernels  127 us (94%)
  local copies, waits for them, and re-layouts  7.63 us (6%)
    pallas_call x1, Pallas kernels, per_device(): return call(blocks, diag_shift.reshape(rows, size), offsets)  127 us
    unnamed x2, local copies, waits for them, and re-layouts  6.35 us

commit v1 on v0

--- a/solution.py
+++ b/solution.py
@@ -12,6 +12,7 @@
 BF16 = jnp.bfloat16
 BW = 4
 LANES = 128
+DIRECT = 2
 
 
 def mm(lhs, rhs):
@@ -24,8 +25,9 @@
     n_slab, n_grp,
     blocks, shift, offs, out,
     w0, l0, w1, l1, wo, lo,
-    base, msg, above, below, reach, sc, rs, rd,
+    base, diag0, relay, msg, above, below, reach, sc, rs, rd,
     in_sem, out_sem, m_send, m_recv, x_send, x_recv, y_send, y_recv, q_send, q_recv,
+    o_send, o_recv, r_send, r_recv,
 ):
     rows, _, size, _ = blocks.shape
     half = size // 2
@@ -36,6 +38,23 @@
     after, before = jnp.minimum(flat + 1, total - 1), jnp.maximum(flat - 1, 0)
     nxt = (after // n_grp, after % n_grp)
     prv = (before // n_grp, before % n_grp)
+
+    n_x, n_zh = n_slab // 2, min(4, n_grp // 2)
+    odd = grp % 2 == 1
+
+    def along_z(place, step):
+        slab_at, grp_at = place
+        z = (grp_at // 2 % n_zh * 2 + slab_at // n_x + step + 4 * n_zh) % (2 * n_zh)
+        return (z % 2 * n_x + slab_at % n_x, grp_at // (2 * n_zh) * (2 * n_zh) + z // 2 * 2 + grp_at % 2)
+
+    my_relay = along_z((slab, grp), -3)
+    origin = along_z((slab, grp), 3)
+    prv_relay = along_z(prv, -3)
+    origin_flat = origin[0] * n_grp + origin[1]
+    target_flat = jnp.minimum(origin_flat + 1, total - 1)
+    target = (target_flat // n_grp, target_flat % n_grp)
+    relaying = jnp.logical_and(odd, origin_flat < total - 1)
+    origin_edge = jnp.logical_and(relaying, origin[1] == n_grp - 1)
     inside = grp < n_grp - 1
     edge_out = jnp.logical_and(has_next, grp == n_grp - 1)
     edge_in = jnp.logical_and(has_prev, grp == 0)
@@ -63,18 +82,49 @@
     def _():
         pl.semaphore_signal(barrier, inc=1, device_id=prv, device_id_type=MESH)
 
-    pl.semaphore_wait(barrier, has_next.astype(jnp.int32) + has_prev.astype(jnp.int32))
-
-    def x_parts(source):
-        parts = []
-        for r in range(rows - 1, -1, -1):
-            first, count = BW - r, r + 1
-            parts.append(remote(source(r, first, count), w0.at[r, pl.ds(first, count)], x_send.at[r], x_recv.at[r], nxt))
-        for r in range(rows - 1, -1, -1):
-            count = BW - r
-            at = rows + r
-            parts.append(remote(source(r, 0, count), w0.at[r, pl.ds(0, count)], x_send.at[at], x_recv.at[at], nxt))
-        return parts
+    @pl.when(odd)
+    def _():
+        pl.semaphore_signal(barrier, inc=1, device_id=origin, device_id_type=MESH)
+
+    from_relay = jnp.logical_and(has_prev, jnp.logical_not(odd))
+
+    @pl.when(from_relay)
+    def _():
+        pl.semaphore_signal(barrier, inc=1, device_id=prv_relay, device_id_type=MESH)
+
+    one = jnp.int32(1)
+    peers = sum(jnp.where(c, one, 0) for c in (has_next, has_prev, odd, relaying))
+    pl.semaphore_wait(barrier, peers)
+
+    def x_crit(source, r, last):
+        first = BW - r
+        cut = pl.ds(first, last - first)
+        return remote(source(r, first, last - first), w0.at[r, cut], x_send.at[r], x_recv.at[r], nxt)
+
+    def x_rest(source, r, first, last):
+        cut = pl.ds(first, last - first)
+        at = rows + r
+        return remote(source(r, first, last - first), w0.at[r, cut], x_send.at[at], x_recv.at[at], nxt)
+
+    downward = list(range(rows - 1, -1, -1))
+    rest = [(r, t) for r in downward for t in range(BW - r)]
+    n_out = len(rest) - DIRECT
+
+    def out_copy(j, source):
+        r, t = rest[j]
+        return remote(source(r, t, 1), relay.at[pl.ds(j, 1)], o_send.at[j], o_recv.at[j], my_relay)
+
+    def on_copy(j):
+        r, t = rest[j]
+        return remote(relay.at[pl.ds(j, 1)], w0.at[r, pl.ds(t, 1)], r_send.at[j], r_recv.at[j], target)
+
+    def forward(js):
+        for j in js:
+
+            @pl.when(relaying if j < n_out else origin_edge)
+            def _():
+                out_copy(j, from_first).wait_recv()
+                on_copy(j).start()
 
     def y_part(row_ref, r, kind):
         at = r * 4 + kind
@@ -95,18 +145,37 @@
             order += [(r, 1)] * (r < rows - 1) + [(r, 2), (r, 3)]
         return [y_part(source(r), r, kind) for r, kind in order]
 
-    from_input = x_parts(lambda r, first, count: blocks.at[r, pl.ds(BW + first, count)])
-    from_first = x_parts(lambda r, first, count: w1.at[BW + r, pl.ds(first, count)])
-    q_copy = remote(blocks.at[:, 2 * BW], base, q_send, q_recv, nxt)
+    def from_input(r, first, count):
+        return blocks.at[r, pl.ds(BW + first, count)]
+
+    def from_first(r, first, count):
+        return w1.at[BW + r, pl.ds(first, count)]
+
+    inside_odd = jnp.logical_and(inside, odd)
+    q_copy = remote(blocks.at[:, 2 * BW], base, q_send.at[0], q_recv.at[0], nxt)
+    g_copy = remote(blocks.at[:, BW], diag0, q_send.at[1], q_recv.at[1], nxt)
 
     @pl.when(inside)
     def _():
-        for part in from_input:
-            part.start()
+        for r in downward:
+            x_crit(from_input, r, BW + 1).start()
+
+    @pl.when(inside_odd)
+    def _():
+        for j in range(n_out):
+            out_copy(j, from_input).start()
+        if DIRECT:
+            x_rest(from_input, 0, BW - DIRECT, BW).start()
+
+    @pl.when(jnp.logical_not(odd))
+    def _():
+        for r in downward:
+            x_rest(from_input, r, 0, BW - r).start()
 
     @pl.when(edge_out)
     def _():
         q_copy.start()
+        g_copy.start()
 
     @pl.when(jnp.logical_not(has_prev))
     def _():
@@ -248,16 +317,21 @@
             keep = reach[pl.ds(r, 1), :] >= float(m)
             l_new[r, k] = jnp.where(jnp.broadcast_to(keep, (size, size)), value, 0.0).astype(BF16)
 
-    def arrive(r, pieces):
+    def arrive(r, pieces, when):
         for c in range(rows):
-
-            @pl.when(jnp.logical_and(has_prev, r == c))
-            def _():
-                for piece in pieces[c]:
-                    piece.wait_recv()
-
-    x_first = [[p] for p in reversed(from_input[:rows])]
-    x_rest = [[p] for p in reversed(from_input[rows:])]
+            if pieces[c]:
+
+                @pl.when(jnp.logical_and(when, r == c))
+                def _():
+                    for piece in pieces[c]:
+                        piece.wait_recv()
+
+    relayed = [[on_copy(j) for j in range(n_out) if rest[j][0] == r] for r in range(rows)]
+    relayed_edge = [[on_copy(j) for j in range(n_out, len(rest)) if rest[j][0] == r] for r in range(rows)]
+    direct_rest = [[x_rest(from_first, 0, BW - DIRECT, BW)] if DIRECT and r == 0 else [] for r in range(rows)]
+    beside_rest = [[x_rest(from_first, r, 0, BW - r)] for r in range(rows)]
+    x_first = [[x_crit(from_first, r, BW + 1)] for r in range(rows)]
+    x_first_edge = [[x_crit(from_first, r, BW)] if r else [] for r in range(rows)]
     y_first = [[y_part(w1.at[BW + r], r, 0)] if r else [] for r in range(rows)]
     y_rest = [
         [y_part(w1.at[BW + r], r, kind) for kind in ((1, 2, 3) if r < rows - 1 else (2, 3))] for r in range(rows)
@@ -266,10 +340,17 @@
     @pl.when(edge_in)
     def _():
         q_copy.wait_recv()
+        g_copy.wait_recv()
+
+    def last_column(r, diag_block, old):
+        keep = above[pl.ds(rows + r, 1), :] >= float(BW)
+        value = base[r].astype(F32) - mm([keep_if(strict_low, diag_block)], [old])
+        return jnp.where(jnp.broadcast_to(keep, (size, size)), value, 0.0).astype(BF16)
 
     def upper_1(i, c):
         r = rows - 1 - i
-        arrive(r, x_first)
+        arrive(r, x_first, grp > 0)
+        arrive(r, x_first_edge, edge_in)
 
         @pl.when(grp > 0)
         def _():
@@ -280,6 +361,8 @@
         def _():
             keep = above[pl.ds(rows + r, 1), :] >= float(BW)
             base[r] = scaled(base[r], r, r + BW, keep)
+            first_diag = scaled_diag(diag0[r], r, above[pl.ds(r, 1), :])
+            w0[r, BW] = last_column(r, first_diag, base[r])
 
         upper_row(r, w0, l0, w1, BW + r)
         return c
@@ -288,6 +371,7 @@
     def _():
         def clear(a, c):
             base[a] = jnp.zeros((size, size), BF16)
+            diag0[a] = jnp.zeros((size, size), BF16)
             return c
 
         lax.fori_loop(0, rows, clear, 0)
@@ -301,12 +385,17 @@
 
     @pl.when(edge_out)
     def _():
-        for part in from_first:
-            part.start()
+        for r in range(rows - 1, 0, -1):
+            x_crit(from_first, r, BW).start()
+        for j in range(len(rest)):
+            out_copy(j, from_first).start()
 
     def lower_1(i, c):
         r = rows - 1 - i
-        arrive(r, x_rest)
+        arrive(r, beside_rest, odd)
+        arrive(r, relayed, from_relay)
+        arrive(r, relayed_edge, edge_in)
+        arrive(r, direct_rest, jnp.logical_and(from_relay, grp > 0))
 
         @pl.when(grp > 0)
         def _():
@@ -319,6 +408,13 @@
 
     lax.fori_loop(0, rows, lower_1, 0)
 
+    half_way = len(rest) // 2
+    forward(range(half_way))
+
+    @pl.when(grp < n_grp - 1)
+    def _():
+        forward(range(half_way, len(rest)))
+
     outs_up = [pltpu.make_async_copy(wo.at[r], out.at[r, pl.ds(BW, BW + 1)], out_sem.at[r]) for r in range(rows)]
     outs_low = [pltpu.make_async_copy(lo.at[r], out.at[r, pl.ds(0, BW)], out_sem.at[rows + r]) for r in range(rows)]
 
@@ -331,10 +427,8 @@
 
     def upper_2(i, c):
         r = rows - 1 - i
-        arrive(r, y_first)
-        keep = above[pl.ds(rows + r, 1), :] >= float(BW)
-        value = base[r].astype(F32) - mm([keep_if(strict_low, w0[r, 0])], [w0[r, BW]])
-        w1[r, BW] = jnp.where(jnp.broadcast_to(keep, (size, size)), value, 0.0).astype(BF16)
+        arrive(r, y_first, has_prev)
+        w1[r, BW] = last_column(r, w0[r, 0], w0[r, BW])
         upper_row(r, w1, l1, wo, r)
         return c
 
@@ -345,12 +439,16 @@
         for part in y_parts(lambda r: wo.at[r]):
             part.start()
 
+    @pl.when(grp == n_grp - 1)
+    def _():
+        forward(range(half_way, len(rest)))
+
     for copy in outs_up:
         copy.start()
 
     def lower_2(i, c):
         r = rows - 1 - i
-        arrive(r, y_rest)
+        arrive(r, y_rest, has_prev)
         rd[pl.ds(r, 1), :] = 1.0 / diagonal(w1[r, 0])
         lower_row(r, w1, l1, lo)
         leave(r, outs_low)
@@ -360,12 +458,40 @@
 
     @pl.when(has_next)
     def _():
-        for part in from_input + y_parts(lambda r: w1.at[BW + r]) + [to_next]:
+        for part in y_parts(lambda r: w1.at[BW + r]) + [to_next]:
             part.wait_send()
 
+    @pl.when(inside)
+    def _():
+        for r in downward:
+            x_crit(from_first, r, BW + 1).wait_send()
+
+    @pl.when(jnp.logical_not(odd))
+    def _():
+        for r in downward:
+            x_rest(from_first, r, 0, BW - r).wait_send()
+
+    @pl.when(inside_odd)
+    def _():
+        for j in range(n_out):
+            out_copy(j, from_first).wait_send()
+        if DIRECT:
+            x_rest(from_first, 0, BW - DIRECT, BW).wait_send()
+
     @pl.when(edge_out)
     def _():
         q_copy.wait_send()
+        g_copy.wait_send()
+        for r in range(rows - 1, 0, -1):
+            x_crit(from_first, r, BW).wait_send()
+        for j in range(len(rest)):
+            out_copy(j, from_first).wait_send()
+
+    for j in range(len(rest)):
+
+        @pl.when(relaying if j < n_out else origin_edge)
+        def _():
+            on_copy(j).wait_send()
 
     @pl.when(has_prev)
     def _():
@@ -378,6 +504,7 @@
 def per_device(n_slab, n_grp, blocks, diag_shift, offsets):
     rows, band, size, _ = blocks.shape
     block = (size, size)
+    n_rest = BW * (BW + 1) // 2
     call = pl.pallas_call(
         functools.partial(kernel, n_slab, n_grp),
         out_shape=jax.ShapeDtypeStruct(blocks.shape, BF16),
@@ -395,6 +522,8 @@
             pltpu.VMEM((rows, BW + 1) + block, BF16),
             pltpu.VMEM((rows, BW) + block, BF16),
             pltpu.VMEM((rows,) + block, BF16),
+            pltpu.VMEM((rows,) + block, BF16),
+            pltpu.VMEM((n_rest,) + block, BF16),
             pltpu.VMEM((2 * rows, size), F32),
             pltpu.VMEM((2 * rows, size), F32),
             pltpu.VMEM((2 * rows, size), F32),
@@ -410,9 +539,9 @@
             pltpu.SemaphoreType.DMA((2 * rows,)),
             pltpu.SemaphoreType.DMA((4 * rows,)),
             pltpu.SemaphoreType.DMA((4 * rows,)),
-            pltpu.SemaphoreType.DMA,
-            pltpu.SemaphoreType.DMA,
-        ],
+            pltpu.SemaphoreType.DMA((2,)),
+            pltpu.SemaphoreType.DMA((2,)),
+        ] + [pltpu.SemaphoreType.DMA((n_rest,))] * 4,
         compiler_params=pltpu.CompilerParams(
             collective_id=0, has_side_effects=True, vmem_limit_bytes=60 * 1024 * 1024
         ),

time: 135 us -> 113 us (0.84)
  Pallas kernels: 127 us -> 105 us
    pallas_call x1, Pallas kernels: 127 us -> 105 us  [per_device(): return call(blocks, diag_shift.reshape(rows, size), offsets)]
where the time goes in v1:
time: 113 us
  Pallas kernels  105 us (93%)
  local copies, waits for them, and re-layouts  7.63 us (7%)
    pallas_call x1, Pallas kernels, per_device(): return call(blocks, diag_shift.reshape(rows, size), offsets)  105 us
    unnamed x2, local copies, waits for them, and re-layouts  6.35 us

profile of v1, /device:TPU:38, one launch (start us, length us, event | category | flops | bytes accessed | tf_op | source)
XLA Modules:
  0.0 112.6 jit_solution(5097778410945628870)
XLA Ops:
  0.0 1.3 %copy.4.offs = s32[4,2]{1,0:T(4,128)} copy(s32[4,2]{0,1:T(2,128)} %param.5) | data formatting | bytes 64 | tf_op args[2]
  1.3 1.3 %reshape.3.shift = f32[4,256]{1,0:T(4,128)} reshape(f32[1024]{0:T(1024)} %param.4) | data formatting | bytes 8192 | tf_op jit(solution)/shard_map/reshape | solution.py:550
  2.6 104.9 %sweeps.1 = bf16[4,9,256,256]{3,2,1,0:T(8,128)(2,1)} custom-call(bf16[4,9,256,256]{3,2,1,0:T(8,128)(2,1)} %blocks.1, f32[4,256]{1,0:T(4,128)} %reshape.3.shift, s32[4,2]{1,0:T(4,128)} %copy.4.offs), custom_call_target="tpu_custom_call" | custom-call | tf_op jit(solution)/shard_map/sweeps/pallas_call | solution.py:550
  107.6 5.0 %copy.6 = bf16[4,9,256,256]{3,2,1,0:T(8,128)(2,1)} copy(bf16[4,9,256,256]{3,2,1,0:T(8,128)(2,1)} %sweeps.1) | data formatting | bytes 9437184

commit v2 on v1

--- a/solution.py
+++ b/solution.py
@@ -23,13 +23,14 @@
 
 def kernel(
     n_slab, n_grp,
-    blocks, shift, offs, out,
-    w0, l0, w1, l1, wo, lo,
-    base, diag0, relay, msg, above, below, reach, sc, rs, rd,
-    in_sem, out_sem, m_send, m_recv, x_send, x_recv, y_send, y_recv, q_send, q_recv,
+    blocks, shift_in, offs_in, out,
+    w0, l0, w1, l1,
+    base, diag0, relay, shift, offs, msg, above, below, reach, sc, rs, rd,
+    in_sem, m_send, m_recv, x_send, x_recv, y_send, y_recv, g_send, g_recv,
     o_send, o_recv, r_send, r_recv,
 ):
     rows, _, size, _ = blocks.shape
+    wo, lo = out.at[:, pl.ds(BW, BW + 1)], out.at[:, pl.ds(0, BW)]
     half = size // 2
     slab, grp = lax.axis_index("slab"), lax.axis_index("grp")
     flat = slab * n_grp + grp
@@ -68,6 +69,8 @@
         pltpu.make_async_copy(blocks.at[:, BW], w0.at[pl.ds(BW, rows), 0], in_sem.at[0]),
         pltpu.make_async_copy(blocks.at[:, pl.ds(BW + 1, BW)], w0.at[pl.ds(BW, rows), pl.ds(1, BW)], in_sem.at[1]),
         pltpu.make_async_copy(blocks.at[:, pl.ds(0, BW)], l0, in_sem.at[2]),
+        pltpu.make_async_copy(shift_in, shift, in_sem.at[3]),
+        pltpu.make_async_copy(offs_in, offs, in_sem.at[4]),
     ]
     for load in loads:
         load.start()
@@ -106,25 +109,43 @@
         at = rows + r
         return remote(source(r, first, last - first), w0.at[r, cut], x_send.at[at], x_recv.at[at], nxt)
 
+    def from_input(r, first, count):
+        return blocks.at[r, pl.ds(BW + first, count)]
+
+    def from_first(r, first, count):
+        return w1.at[BW + r, pl.ds(first, count)]
+
     downward = list(range(rows - 1, -1, -1))
     rest = [(r, t) for r in downward for t in range(BW - r)]
-    n_out = len(rest) - DIRECT
-
-    def out_copy(j, source):
-        r, t = rest[j]
-        return remote(source(r, t, 1), relay.at[pl.ds(j, 1)], o_send.at[j], o_recv.at[j], my_relay)
-
-    def on_copy(j):
-        r, t = rest[j]
-        return remote(relay.at[pl.ds(j, 1)], w0.at[r, pl.ds(t, 1)], r_send.at[j], r_recv.at[j], target)
+    by_relay = rest[: len(rest) - DIRECT]
+    by_relay_edge = [(r, -1) for r in downward] + [(r, t) for r, t in rest if r > 0]
+    n_plain, n_edge = len(by_relay), len(by_relay_edge)
+
+    def out_copy(j, edge, source=from_first):
+        r, t = by_relay_edge[j] if edge else by_relay[j]
+        src = blocks.at[r, pl.ds(2 * BW, 1)] if t < 0 else source(r, t, 1)
+        return remote(src, relay.at[pl.ds(j, 1)], o_send.at[j], o_recv.at[j], my_relay)
+
+    def on_copy(j, edge):
+        r, t = by_relay_edge[j] if edge else by_relay[j]
+        dst = base.at[pl.ds(r, 1)] if t < 0 else w0.at[r, pl.ds(t, 1)]
+        return remote(relay.at[pl.ds(j, 1)], dst, r_send.at[j], r_recv.at[j], target)
+
+    relaying_plain = jnp.logical_and(relaying, jnp.logical_not(origin_edge))
 
     def forward(js):
         for j in js:
-
-            @pl.when(relaying if j < n_out else origin_edge)
+            if j < n_plain:
+
+                @pl.when(relaying_plain)
+                def _():
+                    out_copy(j, False).wait_recv()
+                    on_copy(j, False).start()
+
+            @pl.when(origin_edge)
             def _():
-                out_copy(j, from_first).wait_recv()
-                on_copy(j).start()
+                out_copy(j, True).wait_recv()
+                on_copy(j, True).start()
 
     def y_part(row_ref, r, kind):
         at = r * 4 + kind
@@ -145,37 +166,26 @@
             order += [(r, 1)] * (r < rows - 1) + [(r, 2), (r, 3)]
         return [y_part(source(r), r, kind) for r, kind in order]
 
-    def from_input(r, first, count):
-        return blocks.at[r, pl.ds(BW + first, count)]
-
-    def from_first(r, first, count):
-        return w1.at[BW + r, pl.ds(first, count)]
-
     inside_odd = jnp.logical_and(inside, odd)
-    q_copy = remote(blocks.at[:, 2 * BW], base, q_send.at[0], q_recv.at[0], nxt)
-    g_copy = remote(blocks.at[:, BW], diag0, q_send.at[1], q_recv.at[1], nxt)
-
-    @pl.when(inside)
-    def _():
-        for r in downward:
-            x_crit(from_input, r, BW + 1).start()
+    half_rows = pl.ds(half, half)
+    g_copies = [
+        remote(blocks.at[:, BW, half_rows], diag0.at[:, half_rows], g_send.at[0], g_recv.at[0], nxt),
+        remote(
+            blocks.at[:, BW, pl.ds(0, half), pl.ds(0, half)],
+            diag0.at[:, pl.ds(0, half), pl.ds(0, half)],
+            g_send.at[1], g_recv.at[1], nxt,
+        ),
+    ]
 
     @pl.when(inside_odd)
     def _():
-        for j in range(n_out):
-            out_copy(j, from_input).start()
-        if DIRECT:
-            x_rest(from_input, 0, BW - DIRECT, BW).start()
-
-    @pl.when(jnp.logical_not(odd))
-    def _():
-        for r in downward:
-            x_rest(from_input, r, 0, BW - r).start()
+        for j in range(n_plain):
+            out_copy(j, False, from_input).start()
 
     @pl.when(edge_out)
     def _():
-        q_copy.start()
-        g_copy.start()
+        for j in range(rows):
+            out_copy(j, True).start()
 
     @pl.when(jnp.logical_not(has_prev))
     def _():
@@ -201,11 +211,14 @@
         return jnp.sum(jnp.where(eye, block.astype(F32), 0.0), axis=0, keepdims=True)
 
     loads[0].wait()
+    loads[3].wait()
+    loads[4].wait()
+    reaches = offs[...]
     for r in range(rows):
-        msg[pl.ds(r, 1), :] = shift[pl.ds(r, 1), :] + diagonal(w0[BW + r, 0])
+        msg[pl.ds(r, 1), :] = shift[pl.ds(r * size, size)].reshape(1, size) + diagonal(w0[BW + r, 0])
         at = flat * rows + r
-        up = jnp.minimum(offs[r, 1], total * rows - 1 - at)
-        down = jnp.minimum(offs[r, 0], at)
+        up = jnp.minimum(reaches[1:2, r : r + 1], total * rows - 1 - at)
+        down = jnp.minimum(reaches[0:1, r : r + 1], at)
         msg[pl.ds(rows + r, 1), :] = jnp.broadcast_to(up.astype(F32), (1, size))
         reach[pl.ds(r, 1), :] = jnp.broadcast_to(down.astype(F32), (1, size))
     to_next = remote(msg, above, m_send.at[0], m_recv.at[0], nxt)
@@ -218,6 +231,25 @@
     @pl.when(has_prev)
     def _():
         to_prev.start()
+
+    @pl.when(inside)
+    def _():
+        for r in downward:
+            x_crit(from_input, r, BW + 1).start()
+
+    @pl.when(inside_odd)
+    def _():
+        x_rest(from_input, 0, BW - DIRECT, BW).start()
+
+    @pl.when(jnp.logical_not(odd))
+    def _():
+        for r in downward:
+            x_rest(from_input, r, 0, BW - r).start()
+
+    @pl.when(edge_out)
+    def _():
+        for copy in g_copies:
+            copy.start()
 
     loads[1].wait()
     loads[2].wait()
@@ -326,9 +358,11 @@
                     for piece in pieces[c]:
                         piece.wait_recv()
 
-    relayed = [[on_copy(j) for j in range(n_out) if rest[j][0] == r] for r in range(rows)]
-    relayed_edge = [[on_copy(j) for j in range(n_out, len(rest)) if rest[j][0] == r] for r in range(rows)]
-    direct_rest = [[x_rest(from_first, 0, BW - DIRECT, BW)] if DIRECT and r == 0 else [] for r in range(rows)]
+    relayed = [[on_copy(j, False) for j in range(n_plain) if by_relay[j][0] == r] for r in range(rows)]
+    relayed_edge = [[on_copy(j, True) for j in range(rows, n_edge) if by_relay_edge[j][0] == r] for r in range(rows)]
+    relayed_base = [[on_copy(rows - 1 - r, True)] for r in range(rows)]
+    direct_rest = [[x_rest(from_first, 0, BW - DIRECT, BW)] if r == 0 else [] for r in range(rows)]
+    direct_rest_edge = [[x_rest(from_first, 0, 0, BW)] if r == 0 else [] for r in range(rows)]
     beside_rest = [[x_rest(from_first, r, 0, BW - r)] for r in range(rows)]
     x_first = [[x_crit(from_first, r, BW + 1)] for r in range(rows)]
     x_first_edge = [[x_crit(from_first, r, BW)] if r else [] for r in range(rows)]
@@ -339,8 +373,8 @@
 
     @pl.when(edge_in)
     def _():
-        q_copy.wait_recv()
-        g_copy.wait_recv()
+        for copy in g_copies:
+            copy.wait_recv()
 
     def last_column(r, diag_block, old):
         keep = above[pl.ds(rows + r, 1), :] >= float(BW)
@@ -351,6 +385,7 @@
         r = rows - 1 - i
         arrive(r, x_first, grp > 0)
         arrive(r, x_first_edge, edge_in)
+        arrive(r, relayed_base, edge_in)
 
         @pl.when(grp > 0)
         def _():
@@ -378,7 +413,7 @@
 
     lax.fori_loop(0, rows, upper_1, 0)
 
-    @pl.when(inside)
+    @pl.when(jnp.logical_not(odd))
     def _():
         for part in y_parts(lambda r: w1.at[BW + r]):
             part.start()
@@ -387,15 +422,18 @@
     def _():
         for r in range(rows - 1, 0, -1):
             x_crit(from_first, r, BW).start()
-        for j in range(len(rest)):
-            out_copy(j, from_first).start()
+        for j in range(rows, n_edge):
+            out_copy(j, True).start()
+        x_rest(from_first, 0, 0, BW).start()
 
     def lower_1(i, c):
         r = rows - 1 - i
         arrive(r, beside_rest, odd)
-        arrive(r, relayed, from_relay)
+        plain = jnp.logical_and(from_relay, grp > 0)
+        arrive(r, relayed, plain)
+        arrive(r, direct_rest, plain)
         arrive(r, relayed_edge, edge_in)
-        arrive(r, direct_rest, jnp.logical_and(from_relay, grp > 0))
+        arrive(r, direct_rest_edge, edge_in)
 
         @pl.when(grp > 0)
         def _():
@@ -408,22 +446,18 @@
 
     lax.fori_loop(0, rows, lower_1, 0)
 
-    half_way = len(rest) // 2
+    half_way = n_edge // 2
     forward(range(half_way))
 
+    @pl.when(inside_odd)
+    def _():
+        for part in y_parts(lambda r: w1.at[BW + r]):
+            part.start()
+
+
     @pl.when(grp < n_grp - 1)
     def _():
-        forward(range(half_way, len(rest)))
-
-    outs_up = [pltpu.make_async_copy(wo.at[r], out.at[r, pl.ds(BW, BW + 1)], out_sem.at[r]) for r in range(rows)]
-    outs_low = [pltpu.make_async_copy(lo.at[r], out.at[r, pl.ds(0, BW)], out_sem.at[rows + r]) for r in range(rows)]
-
-    def leave(r, copies):
-        for c in range(rows):
-
-            @pl.when(r == c)
-            def _():
-                copies[c].start()
+        forward(range(half_way, n_edge))
 
     def upper_2(i, c):
         r = rows - 1 - i
@@ -441,17 +475,13 @@
 
     @pl.when(grp == n_grp - 1)
     def _():
-        forward(range(half_way, len(rest)))
-
-    for copy in outs_up:
-        copy.start()
+        forward(range(half_way, n_edge))
 
     def lower_2(i, c):
         r = rows - 1 - i
         arrive(r, y_rest, has_prev)
         rd[pl.ds(r, 1), :] = 1.0 / diagonal(w1[r, 0])
         lower_row(r, w1, l1, lo)
-        leave(r, outs_low)
         return c
 
     lax.fori_loop(0, rows, lower_2, 0)
@@ -473,32 +503,33 @@
 
     @pl.when(inside_odd)
     def _():
-        for j in range(n_out):
-            out_copy(j, from_first).wait_send()
-        if DIRECT:
-            x_rest(from_first, 0, BW - DIRECT, BW).wait_send()
+        for j in range(n_plain):
+            out_copy(j, False).wait_send()
+        x_rest(from_first, 0, BW - DIRECT, BW).wait_send()
 
     @pl.when(edge_out)
     def _():
-        q_copy.wait_send()
-        g_copy.wait_send()
+        for copy in g_copies:
+            copy.wait_send()
         for r in range(rows - 1, 0, -1):
             x_crit(from_first, r, BW).wait_send()
-        for j in range(len(rest)):
-            out_copy(j, from_first).wait_send()
-
-    for j in range(len(rest)):
-
-        @pl.when(relaying if j < n_out else origin_edge)
-        def _():
-            on_copy(j).wait_send()
+        for j in range(n_edge):
+            out_copy(j, True).wait_send()
+        x_rest(from_first, 0, 0, BW).wait_send()
+
+    @pl.when(relaying_plain)
+    def _():
+        for j in range(n_plain):
+            on_copy(j, False).wait_send()
+
+    @pl.when(origin_edge)
+    def _():
+        for j in range(n_edge):
+            on_copy(j, True).wait_send()
 
     @pl.when(has_prev)
     def _():
         to_prev.wait_send()
-
-    for copy in outs_up + outs_low:
-        copy.wait()
 
 
 def per_device(n_slab, n_grp, blocks, diag_shift, offsets):
@@ -507,23 +538,23 @@
     n_rest = BW * (BW + 1) // 2
     call = pl.pallas_call(
         functools.partial(kernel, n_slab, n_grp),
-        out_shape=jax.ShapeDtypeStruct(blocks.shape, BF16),
+        out_shape=pltpu.VMEM(blocks.shape, BF16),
         in_specs=[
-            pl.BlockSpec(memory_space=pl.ANY),
-            pl.BlockSpec(memory_space=pltpu.VMEM),
-            pl.BlockSpec(memory_space=pltpu.SMEM),
+            pl.BlockSpec(memory_space=pltpu.HBM),
+            pl.BlockSpec(memory_space=pltpu.HBM),
+            pl.BlockSpec(memory_space=pltpu.HBM),
         ],
-        out_specs=pl.BlockSpec(memory_space=pl.ANY),
+        out_specs=pl.BlockSpec(memory_space=pltpu.VMEM),
         scratch_shapes=[
             pltpu.VMEM((2 * rows, BW + 1) + block, BF16),
             pltpu.VMEM((rows, BW) + block, BF16),
             pltpu.VMEM((2 * rows, BW + 1) + block, BF16),
             pltpu.VMEM((rows, BW) + block, BF16),
-            pltpu.VMEM((rows, BW + 1) + block, BF16),
-            pltpu.VMEM((rows, BW) + block, BF16),
             pltpu.VMEM((rows,) + block, BF16),
             pltpu.VMEM((rows,) + block, BF16),
             pltpu.VMEM((n_rest,) + block, BF16),
+            pltpu.VMEM((rows * size,), F32),
+            pltpu.VMEM((2, rows), jnp.int32),
             pltpu.VMEM((2 * rows, size), F32),
             pltpu.VMEM((2 * rows, size), F32),
             pltpu.VMEM((2 * rows, size), F32),
@@ -531,8 +562,7 @@
             pltpu.VMEM((4 * rows, size), F32),
             pltpu.VMEM((2 * rows, size, LANES), F32),
             pltpu.VMEM((2 * rows, size), F32),
-            pltpu.SemaphoreType.DMA((3,)),
-            pltpu.SemaphoreType.DMA((2 * rows,)),
+            pltpu.SemaphoreType.DMA((5,)),
             pltpu.SemaphoreType.DMA((2,)),
             pltpu.SemaphoreType.DMA((2,)),
             pltpu.SemaphoreType.DMA((2 * rows,)),
@@ -543,11 +573,11 @@
             pltpu.SemaphoreType.DMA((2,)),
         ] + [pltpu.SemaphoreType.DMA((n_rest,))] * 4,
         compiler_params=pltpu.CompilerParams(
-            collective_id=0, has_side_effects=True, vmem_limit_bytes=60 * 1024 * 1024
+            collective_id=0, has_side_effects=True, vmem_limit_bytes=67_043_328 - 2 * blocks.size
         ),
         name="sweeps",
     )
-    return call(blocks, diag_shift.reshape(rows, size), offsets)
+    return call(blocks, diag_shift, offsets.T)
 
 
 def solution(mesh):

time: 113 us -> 102 us (0.903)
  local copies, waits for them, and re-layouts: 7.63 us -> 2.19 us
  Pallas kernels: 105 us -> 99.8 us
    pallas_call x1, Pallas kernels: 105 us -> 99.8 us  [per_device(): return call(blocks, diag_shift, offsets.T)]
    unnamed x2 -> x1, local copies, waits for them, and re-layouts: 6.35 us -> 2.19 us
    reshape x1 -> x0, local copies, waits for them, and re-layouts: 1.29 us -> none  [per_device(): return call(blocks, diag_shift.reshape(rows, size), offsets)]
where the time goes in v2:
time: 102 us
  Pallas kernels  99.8 us (98%)
  local copies, waits for them, and re-layouts  2.19 us (2%)
    pallas_call x1, Pallas kernels, per_device(): return call(blocks, diag_shift, offsets.T)  99.8 us
    unnamed x1, local copies, waits for them, and re-layouts  2.19 us

profile of v2, /device:TPU:38, one launch (start us, length us, event | category | flops | bytes accessed | tf_op | source)
XLA Modules:
  0.0 102.0 jit_solution(16671381513156634639)
XLA Ops:
  0.0 99.8 %sweeps.1 = bf16[4,9,256,256]{3,2,1,0:T(8,128)(2,1)S(1)} custom-call(bf16[4,9,256,256]{3,2,1,0:T(8,128)(2,1)} %blocks.1, f32[1024]{0:T(1024)} %shift_in.1, s32[2,4]{1,0:T(2,128)} %bitcast.1), custom_call_target="tpu_custom_call" | custom-call | tf_op jit(solution)/shard_map/sweeps/pallas_call | solution.py:580
  99.8 2.2 %copy.5 = bf16[4,9,256,256]{3,2,1,0:T(8,128)(2,1)} copy(bf16[4,9,256,256]{3,2,1,0:T(8,128)(2,1)S(1)} %sweeps.1) | data formatting | bytes 9437184

commit v3 on v2

--- a/solution.py
+++ b/solution.py
@@ -13,6 +13,7 @@
 BW = 4
 LANES = 128
 DIRECT = 2
+DIRECT_EDGE = 1
 
 
 def mm(lhs, rhs):
@@ -25,7 +26,7 @@
     n_slab, n_grp,
     blocks, shift_in, offs_in, out,
     w0, l0, w1, l1,
-    base, diag0, relay, shift, offs, msg, above, below, reach, sc, rs, rd,
+    base, diag0, relay, packed, corner, corner_in, shift, offs, msg, above, below, reach, sc, rs, rd,
     in_sem, m_send, m_recv, x_send, x_recv, y_send, y_recv, g_send, g_recv,
     o_send, o_recv, r_send, r_recv,
 ):
@@ -117,58 +118,46 @@
 
     downward = list(range(rows - 1, -1, -1))
     rest = [(r, t) for r in downward for t in range(BW - r)]
-    by_relay = rest[: len(rest) - DIRECT]
-    by_relay_edge = [(r, -1) for r in downward] + [(r, t) for r, t in rest if r > 0]
-    n_plain, n_edge = len(by_relay), len(by_relay_edge)
-
-    def out_copy(j, edge, source=from_first):
-        r, t = by_relay_edge[j] if edge else by_relay[j]
-        src = blocks.at[r, pl.ds(2 * BW, 1)] if t < 0 else source(r, t, 1)
-        return remote(src, relay.at[pl.ds(j, 1)], o_send.at[j], o_recv.at[j], my_relay)
-
-    def on_copy(j, edge):
-        r, t = by_relay_edge[j] if edge else by_relay[j]
-        dst = base.at[pl.ds(r, 1)] if t < 0 else w0.at[r, pl.ds(t, 1)]
-        return remote(relay.at[pl.ds(j, 1)], dst, r_send.at[j], r_recv.at[j], target)
+    n_plain, n_edge = len(rest) - DIRECT, len(rest) - DIRECT_EDGE
+
+    def out_copy(j, source=from_first):
+        r, t = rest[j]
+        return remote(source(r, t, 1), relay.at[pl.ds(j, 1)], o_send.at[j], o_recv.at[j], my_relay)
+
+    def on_copy(j):
+        r, t = rest[j]
+        return remote(relay.at[pl.ds(j, 1)], w0.at[r, pl.ds(t, 1)], r_send.at[j], r_recv.at[j], target)
 
     relaying_plain = jnp.logical_and(relaying, jnp.logical_not(origin_edge))
 
     def forward(js):
         for j in js:
-            if j < n_plain:
-
-                @pl.when(relaying_plain)
-                def _():
-                    out_copy(j, False).wait_recv()
-                    on_copy(j, False).start()
-
-            @pl.when(origin_edge)
+
+            @pl.when(relaying_plain if j >= n_edge else origin_edge if j >= n_plain else relaying)
             def _():
-                out_copy(j, True).wait_recv()
-                on_copy(j, True).start()
+                out_copy(j).wait_recv()
+                on_copy(j).start()
 
     def y_part(row_ref, r, kind):
-        at = r * 4 + kind
-        dst = w1.at[r]
-        if kind == 0:
-            cut = (pl.ds(BW - r, r),)
-        elif kind == 1:
-            cut = (pl.ds(1, BW - 1 - r),)
-        elif kind == 2:
-            cut = (0, pl.ds(0, half))
-        else:
-            cut = (0, pl.ds(half, half), pl.ds(half, half))
-        return remote(row_ref.at[cut], dst.at[cut], y_send.at[at], y_recv.at[at], nxt)
+        at = r * 3 + kind
+        sems = (y_send.at[at], y_recv.at[at], nxt)
+        if kind == 2:
+            return remote(packed.at[r], w1.at[r, 0, pl.ds(0, half)], *sems)
+        cut = pl.ds(1, BW - 1 - r) if kind else pl.ds(BW - r, r)
+        return remote(row_ref.at[cut], w1.at[r, cut], *sems)
+
+    corner_copy = remote(corner, corner_in, y_send.at[3 * rows], y_recv.at[3 * rows], nxt)
 
     def y_parts(source):
         order = [(r, 0) for r in range(rows - 1, 0, -1)]
         for r in range(rows - 1, -1, -1):
-            order += [(r, 1)] * (r < rows - 1) + [(r, 2), (r, 3)]
-        return [y_part(source(r), r, kind) for r, kind in order]
+            order += [(r, 1)] * (r < rows - 1) + [(r, 2)]
+        return [corner_copy] + [y_part(source(r), r, kind) for r, kind in order]
 
     inside_odd = jnp.logical_and(inside, odd)
     half_rows = pl.ds(half, half)
     g_copies = [
+        remote(blocks.at[:, 2 * BW], base, g_send.at[2], g_recv.at[2], nxt),
         remote(blocks.at[:, BW, half_rows], diag0.at[:, half_rows], g_send.at[0], g_recv.at[0], nxt),
         remote(
             blocks.at[:, BW, pl.ds(0, half), pl.ds(0, half)],
@@ -180,12 +169,7 @@
     @pl.when(inside_odd)
     def _():
         for j in range(n_plain):
-            out_copy(j, False, from_input).start()
-
-    @pl.when(edge_out)
-    def _():
-        for j in range(rows):
-            out_copy(j, True).start()
+            out_copy(j, from_input).start()
 
     @pl.when(jnp.logical_not(has_prev))
     def _():
@@ -237,10 +221,6 @@
         for r in downward:
             x_crit(from_input, r, BW + 1).start()
 
-    @pl.when(inside_odd)
-    def _():
-        x_rest(from_input, 0, BW - DIRECT, BW).start()
-
     @pl.when(jnp.logical_not(odd))
     def _():
         for r in downward:
@@ -301,6 +281,7 @@
 
     def own_diag(r, c):
         w0[BW + r, 0] = scaled_diag(w0[BW + r, 0], BW + r, msg[pl.ds(r, 1), :])
+        rd[pl.ds(BW + r, 1), :] = 1.0 / diagonal(w0[BW + r, 0])
         return c
 
     lax.fori_loop(0, rows, own_diag, 0)
@@ -320,11 +301,12 @@
     def keep_if(mask, block):
         return jnp.where(mask, block.astype(F32), 0.0).astype(BF16)
 
-    def upper_row(r, w, l, w_new, new_row):
+    again = 2 * rows
+
+    def upper_row(r, w, l, w_new, new_row, at):
         own = w[BW + r, 0]
         low = keep_if(strict_low, own)
-        pivot = 1.0 / diagonal(own)
-        rd[pl.ds(BW + r, 1), :] = pivot
+        pivot = rd[pl.ds(at + BW + r, 1), :]
         for t in range(BW + 1):
             lhs, rhs = [low], [keep_if(strict_up, own) if t == 0 else w[BW + r, t]]
             for m in range(1, BW + 1 - t):
@@ -338,14 +320,32 @@
                 value = jnp.where(jnp.broadcast_to(keep, (size, size)), value, 0.0)
             w_new[new_row, t] = value.astype(BF16)
 
-    def lower_row(r, w, l, l_new):
+    row_half = lax.broadcasted_iota(jnp.int32, (half, half), 0)
+    col_half = lax.broadcasted_iota(jnp.int32, (half, half), 1)
+    eye_half = row_half == col_half
+    low_half, high_half = pl.ds(0, half), pl.ds(half, half)
+
+    def pack(r, w, row):
+        last = w[row, 0, high_half, high_half].astype(F32)
+        first = jnp.where(col_half >= row_half, w[row, 0, low_half, low_half].astype(F32), last.T)
+        packed[r, :, low_half] = first.astype(BF16)
+        packed[r, :, high_half] = w[row, 0, low_half, high_half]
+        corner[pl.ds(r, 1), :] = jnp.sum(jnp.where(eye_half, last, 0.0), axis=0, keepdims=True)
+
+    def unpack(r):
+        first = w1[r, 0, low_half, low_half].astype(F32)
+        values = jnp.broadcast_to(corner_in[pl.ds(r, 1), :], (half, half))
+        last = jnp.where(col_half > row_half, first.T, jnp.where(eye_half, values, 0.0))
+        w1[r, 0, high_half, high_half] = last.astype(BF16)
+
+    def lower_row(r, w, l, l_new, at):
         for k in range(BW):
             m = BW - k
             lhs, rhs = [l[r, k]], [keep_if(strict_up, w[BW + r - m, 0])]
             for back in range(m + 1, BW + 1):
                 lhs.append(l[r, BW - back])
                 rhs.append(w[BW + r - back, back - m])
-            value = (l0[r, k].astype(F32) - mm(lhs, rhs)) * rd[pl.ds(BW + r - m, 1), :]
+            value = (l0[r, k].astype(F32) - mm(lhs, rhs)) * rd[pl.ds(at + BW + r - m, 1), :]
             keep = reach[pl.ds(r, 1), :] >= float(m)
             l_new[r, k] = jnp.where(jnp.broadcast_to(keep, (size, size)), value, 0.0).astype(BF16)
 
@@ -358,18 +358,20 @@
                     for piece in pieces[c]:
                         piece.wait_recv()
 
-    relayed = [[on_copy(j, False) for j in range(n_plain) if by_relay[j][0] == r] for r in range(rows)]
-    relayed_edge = [[on_copy(j, True) for j in range(rows, n_edge) if by_relay_edge[j][0] == r] for r in range(rows)]
-    relayed_base = [[on_copy(rows - 1 - r, True)] for r in range(rows)]
-    direct_rest = [[x_rest(from_first, 0, BW - DIRECT, BW)] if r == 0 else [] for r in range(rows)]
-    direct_rest_edge = [[x_rest(from_first, 0, 0, BW)] if r == 0 else [] for r in range(rows)]
+    def by_row(js):
+        return [[on_copy(j) for j in js if rest[j][0] == r] for r in range(rows)]
+
+    relayed, relayed_edge = by_row(range(n_plain)), by_row(range(n_edge))
+    direct_rest = [[x_rest(from_first, 0, BW - DIRECT, BW)] if r == 0 and DIRECT else [] for r in range(rows)]
+    direct_rest_edge = [
+        [x_rest(from_first, 0, BW - DIRECT_EDGE, BW)] if r == 0 and DIRECT_EDGE else [] for r in range(rows)
+    ]
     beside_rest = [[x_rest(from_first, r, 0, BW - r)] for r in range(rows)]
     x_first = [[x_crit(from_first, r, BW + 1)] for r in range(rows)]
     x_first_edge = [[x_crit(from_first, r, BW)] if r else [] for r in range(rows)]
     y_first = [[y_part(w1.at[BW + r], r, 0)] if r else [] for r in range(rows)]
-    y_rest = [
-        [y_part(w1.at[BW + r], r, kind) for kind in ((1, 2, 3) if r < rows - 1 else (2, 3))] for r in range(rows)
-    ]
+    y_rest = [[y_part(w1.at[BW + r], r, kind) for kind in ((1, 2) if r < rows - 1 else (2,))] for r in range(rows)]
+    y_rest[rows - 1].append(corner_copy)
 
     @pl.when(edge_in)
     def _():
@@ -385,7 +387,6 @@
         r = rows - 1 - i
         arrive(r, x_first, grp > 0)
         arrive(r, x_first_edge, edge_in)
-        arrive(r, relayed_base, edge_in)
 
         @pl.when(grp > 0)
         def _():
@@ -399,7 +400,9 @@
             first_diag = scaled_diag(diag0[r], r, above[pl.ds(r, 1), :])
             w0[r, BW] = last_column(r, first_diag, base[r])
 
-        upper_row(r, w0, l0, w1, BW + r)
+        upper_row(r, w0, l0, w1, BW + r, 0)
+        rd[pl.ds(again + BW + r, 1), :] = 1.0 / diagonal(w1[BW + r, 0])
+        pack(r, w1, BW + r)
         return c
 
     @pl.when(jnp.logical_not(has_prev))
@@ -422,9 +425,10 @@
     def _():
         for r in range(rows - 1, 0, -1):
             x_crit(from_first, r, BW).start()
-        for j in range(rows, n_edge):
-            out_copy(j, True).start()
-        x_rest(from_first, 0, 0, BW).start()
+        for j in range(n_edge):
+            out_copy(j).start()
+        if DIRECT_EDGE:
+            x_rest(from_first, 0, BW - DIRECT_EDGE, BW).start()
 
     def lower_1(i, c):
         r = rows - 1 - i
@@ -441,50 +445,75 @@
             lax.fori_loop(1, BW - r, above_upper(r), 0)
 
         rd[pl.ds(r, 1), :] = 1.0 / diagonal(w0[r, 0])
-        lower_row(r, w0, l0, l1)
-        return c
-
-    lax.fori_loop(0, rows, lower_1, 0)
-
-    half_way = n_edge // 2
+        lower_row(r, w0, l0, l1, 0)
+        return c
+
+    @pl.when(odd)
+    def _():
+        lax.fori_loop(0, rows, lower_1, 0)
+
+    n_most = max(n_plain, n_edge)
+    half_way = n_most // 2
     forward(range(half_way))
 
     @pl.when(inside_odd)
     def _():
+        x_rest(from_input, 0, BW - DIRECT, BW).start()
         for part in y_parts(lambda r: w1.at[BW + r]):
             part.start()
 
 
     @pl.when(grp < n_grp - 1)
     def _():
-        forward(range(half_way, n_edge))
+        forward(range(half_way, n_most))
 
     def upper_2(i, c):
         r = rows - 1 - i
         arrive(r, y_first, has_prev)
         w1[r, BW] = last_column(r, w0[r, 0], w0[r, BW])
-        upper_row(r, w1, l1, wo, r)
-        return c
-
-    lax.fori_loop(0, rows, upper_2, 0)
-
-    @pl.when(edge_out)
-    def _():
-        for part in y_parts(lambda r: wo.at[r]):
-            part.start()
-
-    @pl.when(grp == n_grp - 1)
-    def _():
-        forward(range(half_way, n_edge))
+        upper_row(r, w1, l1, wo, r, again)
+
+        @pl.when(edge_out)
+        def _():
+            pack(r, wo, r)
+
+        return c
 
     def lower_2(i, c):
         r = rows - 1 - i
         arrive(r, y_rest, has_prev)
-        rd[pl.ds(r, 1), :] = 1.0 / diagonal(w1[r, 0])
-        lower_row(r, w1, l1, lo)
-        return c
-
-    lax.fori_loop(0, rows, lower_2, 0)
+
+        @pl.when(has_prev)
+        def _():
+            unpack(r)
+
+        rd[pl.ds(again + r, 1), :] = 1.0 / diagonal(w1[r, 0])
+        lower_row(r, w1, l1, lo, again)
+        return c
+
+    @pl.when(odd)
+    def _():
+        lax.fori_loop(0, rows, upper_2, 0)
+
+    @pl.when(edge_out)
+    def _():
+        for part in y_parts(lambda r: wo.at[r]):
+            part.start()
+
+    @pl.when(grp == n_grp - 1)
+    def _():
+        forward(range(half_way, n_most))
+
+    def finish(i, c):
+        @pl.when(jnp.logical_not(odd))
+        def _():
+            lower_1(i, c)
+            upper_2(i, c)
+
+        lower_2(i, c)
+        return c
+
+    lax.fori_loop(0, rows, finish, 0)
 
     @pl.when(has_next)
     def _():
@@ -504,7 +533,7 @@
     @pl.when(inside_odd)
     def _():
         for j in range(n_plain):
-            out_copy(j, False).wait_send()
+            out_copy(j).wait_send()
         x_rest(from_first, 0, BW - DIRECT, BW).wait_send()
 
     @pl.when(edge_out)
@@ -514,18 +543,19 @@
         for r in range(rows - 1, 0, -1):
             x_crit(from_first, r, BW).wait_send()
         for j in range(n_edge):
-            out_copy(j, True).wait_send()
-        x_rest(from_first, 0, 0, BW).wait_send()
+            out_copy(j).wait_send()
+        if DIRECT_EDGE:
+            x_rest(from_first, 0, BW - DIRECT_EDGE, BW).wait_send()
 
     @pl.when(relaying_plain)
     def _():
         for j in range(n_plain):
-            on_copy(j, False).wait_send()
+            on_copy(j).wait_send()
 
     @pl.when(origin_edge)
     def _():
         for j in range(n_edge):
-            on_copy(j, True).wait_send()
+            on_copy(j).wait_send()
 
     @pl.when(has_prev)
     def _():
@@ -553,6 +583,9 @@
             pltpu.VMEM((rows,) + block, BF16),
             pltpu.VMEM((rows,) + block, BF16),
             pltpu.VMEM((n_rest,) + block, BF16),
+            pltpu.VMEM((rows, size // 2, size), BF16),
+            pltpu.VMEM((2 * rows, size // 2), F32),
+            pltpu.VMEM((2 * rows, size // 2), F32),
             pltpu.VMEM((rows * size,), F32),
             pltpu.VMEM((2, rows), jnp.int32),
             pltpu.VMEM((2 * rows, size), F32),
@@ -561,7 +594,7 @@
             pltpu.VMEM((2 * rows, size), F32),
             pltpu.VMEM((4 * rows, size), F32),
             pltpu.VMEM((2 * rows, size, LANES), F32),
-            pltpu.VMEM((2 * rows, size), F32),
+            pltpu.VMEM((4 * rows, size), F32),
             pltpu.SemaphoreType.DMA((5,)),
             pltpu.SemaphoreType.DMA((2,)),
             pltpu.SemaphoreType.DMA((2,)),
@@ -569,8 +602,8 @@
             pltpu.SemaphoreType.DMA((2 * rows,)),
             pltpu.SemaphoreType.DMA((4 * rows,)),
             pltpu.SemaphoreType.DMA((4 * rows,)),
-            pltpu.SemaphoreType.DMA((2,)),
-            pltpu.SemaphoreType.DMA((2,)),
+            pltpu.SemaphoreType.DMA((3,)),
+            pltpu.SemaphoreType.DMA((3,)),
         ] + [pltpu.SemaphoreType.DMA((n_rest,))] * 4,
         compiler_params=pltpu.CompilerParams(
             collective_id=0, has_side_effects=True, vmem_limit_bytes=67_043_328 - 2 * blocks.size

time: 102 us -> 96.9 us (0.950)
  Pallas kernels: 99.8 us -> 94.6 us
    pallas_call x1, Pallas kernels: 99.8 us -> 94.6 us  [per_device(): return call(blocks, diag_shift, offsets.T)]
where the time goes in v3:
time: 96.9 us; the launch traced here: 96.8 us
  Pallas kernels  94.6 us (98%)
  local copies, waits for them, and re-layouts  2.19 us (2%)
    pallas_call x1, Pallas kernels, per_device(): return call(blocks, diag_shift, offsets.T)  94.6 us
    unnamed x1, local copies, waits for them, and re-layouts  2.19 us

profile of v3, /device:TPU:38, one launch (start us, length us, event | category | flops | bytes accessed | tf_op | source)
XLA Modules:
  0.0 96.8 jit_solution(13206203855484366062)
XLA Ops:
  0.0 94.6 %sweeps.1 = bf16[4,9,256,256]{3,2,1,0:T(8,128)(2,1)S(1)} custom-call(bf16[4,9,256,256]{3,2,1,0:T(8,128)(2,1)} %blocks.1, f32[1024]{0:T(1024)} %shift_in.1, s32[2,4]{1,0:T(2,128)} %bitcast.1), custom_call_target="tpu_custom_call" | custom-call | tf_op jit(solution)/shard_map/sweeps/pallas_call | solution.py:613
  94.6 2.2 %copy.5 = bf16[4,9,256,256]{3,2,1,0:T(8,128)(2,1)} copy(bf16[4,9,256,256]{3,2,1,0:T(8,128)(2,1)S(1)} %sweeps.1) | data formatting | bytes 9437184

commit v4 on v3

--- a/solution.py
+++ b/solution.py
@@ -13,7 +13,9 @@
 BW = 4
 LANES = 128
 DIRECT = 2
-DIRECT_EDGE = 1
+DIRECT_EDGE = 3
+HEAD = 2
+CHIPS_ZH = 4
 
 
 def mm(lhs, rhs):
@@ -26,9 +28,9 @@
     n_slab, n_grp,
     blocks, shift_in, offs_in, out,
     w0, l0, w1, l1,
-    base, diag0, relay, packed, corner, corner_in, shift, offs, msg, above, below, reach, sc, rs, rd,
+    base, diag0, packed0, side_block, relay, packed, corner, corner_in, shift, offs, msg, above, below, reach, sc, rs, rd,
     in_sem, m_send, m_recv, x_send, x_recv, y_send, y_recv, g_send, g_recv,
-    o_send, o_recv, r_send, r_recv,
+    o_send, o_recv, r_send, r_recv, s_send, s_recv, t_send, t_recv,
 ):
     rows, _, size, _ = blocks.shape
     wo, lo = out.at[:, pl.ds(BW, BW + 1)], out.at[:, pl.ds(0, BW)]
@@ -41,7 +43,7 @@
     nxt = (after // n_grp, after % n_grp)
     prv = (before // n_grp, before % n_grp)
 
-    n_x, n_zh = n_slab // 2, min(4, n_grp // 2)
+    n_x, n_zh = n_slab // 2, min(CHIPS_ZH, n_grp // 2)
     odd = grp % 2 == 1
 
     def along_z(place, step):
@@ -49,14 +51,27 @@
         z = (grp_at // 2 % n_zh * 2 + slab_at // n_x + step + 4 * n_zh) % (2 * n_zh)
         return (z % 2 * n_x + slab_at % n_x, grp_at // (2 * n_zh) * (2 * n_zh) + z // 2 * 2 + grp_at % 2)
 
-    my_relay = along_z((slab, grp), -3)
-    origin = along_z((slab, grp), 3)
-    prv_relay = along_z(prv, -3)
+    def relay_of(place):
+        slab_at, grp_at = along_z(place, -3)
+        return (slab_at, jnp.where(grp_at == n_grp - 1, n_grp - 2, grp_at))
+
+    my_relay, prv_relay = relay_of((slab, grp)), relay_of(prv)
+    is_relay = jnp.logical_or(jnp.logical_and(odd, grp != n_grp - 1), grp == n_grp - 2)
+    origin = along_z((slab, grp // 2 * 2 + 1), 3)
     origin_flat = origin[0] * n_grp + origin[1]
     target_flat = jnp.minimum(origin_flat + 1, total - 1)
     target = (target_flat // n_grp, target_flat % n_grp)
-    relaying = jnp.logical_and(odd, origin_flat < total - 1)
+    relaying = jnp.logical_and(is_relay, origin_flat < total - 1)
     origin_edge = jnp.logical_and(relaying, origin[1] == n_grp - 1)
+
+    n_side = n_grp // (2 * n_zh) - 1
+    side_back = (n_grp - 2 - grp) // (2 * n_zh)
+    on_side = jnp.logical_and(slab < n_slab - 1, (n_grp - 2 - grp) % (2 * n_zh) == 0)
+    on_side = jnp.logical_and(on_side, side_back > 0)
+    edge_after, edge_last = (jnp.minimum(slab + 1, n_slab - 1), 0), (slab, n_grp - 1)
+
+    def side(slab_at, k):
+        return (slab_at, n_grp - 2 - 2 * n_zh * k)
     inside = grp < n_grp - 1
     edge_out = jnp.logical_and(has_next, grp == n_grp - 1)
     edge_in = jnp.logical_and(has_prev, grp == 0)
@@ -86,7 +101,7 @@
     def _():
         pl.semaphore_signal(barrier, inc=1, device_id=prv, device_id_type=MESH)
 
-    @pl.when(odd)
+    @pl.when(is_relay)
     def _():
         pl.semaphore_signal(barrier, inc=1, device_id=origin, device_id_type=MESH)
 
@@ -96,8 +111,18 @@
     def _():
         pl.semaphore_signal(barrier, inc=1, device_id=prv_relay, device_id_type=MESH)
 
+    @pl.when(on_side)
+    def _():
+        pl.semaphore_signal(barrier, inc=1, device_id=edge_last, device_id_type=MESH)
+
+    @pl.when(edge_in)
+    def _():
+        for k in range(1, n_side + 1):
+            pl.semaphore_signal(barrier, inc=1, device_id=side(prv[0], k), device_id_type=MESH)
+
     one = jnp.int32(1)
-    peers = sum(jnp.where(c, one, 0) for c in (has_next, has_prev, odd, relaying))
+    peers = sum(jnp.where(c, one, 0) for c in (has_next, has_prev, odd, relaying, on_side))
+    peers = peers + jnp.where(edge_out, jnp.int32(n_side), 0)
     pl.semaphore_wait(barrier, peers)
 
     def x_crit(source, r, last):
@@ -119,6 +144,7 @@
     downward = list(range(rows - 1, -1, -1))
     rest = [(r, t) for r in downward for t in range(BW - r)]
     n_plain, n_edge = len(rest) - DIRECT, len(rest) - DIRECT_EDGE
+    inside_odd = jnp.logical_and(inside, odd)
 
     def out_copy(j, source=from_first):
         r, t = rest[j]
@@ -128,12 +154,17 @@
         r, t = rest[j]
         return remote(relay.at[pl.ds(j, 1)], w0.at[r, pl.ds(t, 1)], r_send.at[j], r_recv.at[j], target)
 
-    relaying_plain = jnp.logical_and(relaying, jnp.logical_not(origin_edge))
+    relays_plain = jnp.logical_and(relaying, jnp.logical_not(origin_edge))
+    by_kind = ((relays_plain, n_plain), (origin_edge, n_edge))
 
     def forward(js):
         for j in js:
 
-            @pl.when(relaying_plain if j >= n_edge else origin_edge if j >= n_plain else relaying)
+            mine = jnp.bool_(False)
+            for kind, count in by_kind:
+                mine = jnp.logical_or(mine, jnp.logical_and(kind, j < count))
+
+            @pl.when(mine)
             def _():
                 out_copy(j).wait_recv()
                 on_copy(j).start()
@@ -148,28 +179,49 @@
 
     corner_copy = remote(corner, corner_in, y_send.at[3 * rows], y_recv.at[3 * rows], nxt)
 
+    def side_out(k):
+        return remote(wo.at[0, k], side_block.at[0], s_send.at[k - 1], s_recv.at[k - 1], side(slab, k))
+
+    def side_on(k):
+        return remote(side_block.at[0], w1.at[0, k], t_send.at[k - 1], t_recv.at[k - 1], edge_after)
+
+    def y_edge():
+        cut = pl.ds(1 + n_side, BW - 1 - n_side)
+        return [remote(wo.at[0, cut], w1.at[0, cut], y_send.at[1], y_recv.at[1], nxt)] if BW - 1 > n_side else []
+
+    def y_parts_edge():
+        order = [(r, 0) for r in range(rows - 1, 0, -1)]
+        for r in range(rows - 1, 0, -1):
+            order += [(r, 1)] * (r < rows - 1) + [(r, 2)]
+        parts = [y_part(wo.at[r], r, kind) for r, kind in order]
+        return [corner_copy] + parts + y_edge() + [y_part(wo.at[0], 0, 2)]
+
     def y_parts(source):
         order = [(r, 0) for r in range(rows - 1, 0, -1)]
         for r in range(rows - 1, -1, -1):
             order += [(r, 1)] * (r < rows - 1) + [(r, 2)]
         return [corner_copy] + [y_part(source(r), r, kind) for r, kind in order]
 
-    inside_odd = jnp.logical_and(inside, odd)
-    half_rows = pl.ds(half, half)
     g_copies = [
-        remote(blocks.at[:, 2 * BW], base, g_send.at[2], g_recv.at[2], nxt),
-        remote(blocks.at[:, BW, half_rows], diag0.at[:, half_rows], g_send.at[0], g_recv.at[0], nxt),
-        remote(
-            blocks.at[:, BW, pl.ds(0, half), pl.ds(0, half)],
-            diag0.at[:, pl.ds(0, half), pl.ds(0, half)],
-            g_send.at[1], g_recv.at[1], nxt,
-        ),
+        remote(blocks.at[:, 2 * BW], base, g_send.at[0], g_recv.at[0], nxt),
+        remote(packed0, diag0, g_send.at[1], g_recv.at[1], nxt),
     ]
 
     @pl.when(inside_odd)
     def _():
         for j in range(n_plain):
             out_copy(j, from_input).start()
+
+    head = downward[rows - HEAD :]
+
+    @pl.when(inside_odd)
+    def _():
+        for r in head:
+            x_crit(from_input, r, BW + 1).start()
+
+    @pl.when(edge_out)
+    def _():
+        g_copies[0].start()
 
     @pl.when(jnp.logical_not(has_prev))
     def _():
@@ -190,6 +242,11 @@
     row_id = lax.broadcasted_iota(jnp.int32, (size, size), 0)
     col_id = lax.broadcasted_iota(jnp.int32, (size, size), 1)
     eye = row_id == col_id
+
+    row_half = lax.broadcasted_iota(jnp.int32, (half, half), 0)
+    col_half = lax.broadcasted_iota(jnp.int32, (half, half), 1)
+    eye_half = row_half == col_half
+    low_half, high_half = pl.ds(0, half), pl.ds(half, half)
 
     def diagonal(block):
         return jnp.sum(jnp.where(eye, block.astype(F32), 0.0), axis=0, keepdims=True)
@@ -218,7 +275,12 @@
 
     @pl.when(inside)
     def _():
-        for r in downward:
+        for r in downward[: rows - HEAD]:
+            x_crit(from_input, r, BW + 1).start()
+
+    @pl.when(jnp.logical_not(odd))
+    def _():
+        for r in head:
             x_crit(from_input, r, BW + 1).start()
 
     @pl.when(jnp.logical_not(odd))
@@ -228,8 +290,15 @@
 
     @pl.when(edge_out)
     def _():
-        for copy in g_copies:
-            copy.start()
+        def pack_low(r, c):
+            first = w0[BW + r, 0, low_half, low_half].astype(F32)
+            last = w0[BW + r, 0, high_half, high_half].astype(F32)
+            packed0[r, :, low_half] = jnp.where(col_half < row_half, first, last.T).astype(BF16)
+            packed0[r, :, high_half] = w0[BW + r, 0, high_half, low_half]
+            return c
+
+        lax.fori_loop(0, rows, pack_low, 0)
+        g_copies[1].start()
 
     loads[1].wait()
     loads[2].wait()
@@ -320,11 +389,6 @@
                 value = jnp.where(jnp.broadcast_to(keep, (size, size)), value, 0.0)
             w_new[new_row, t] = value.astype(BF16)
 
-    row_half = lax.broadcasted_iota(jnp.int32, (half, half), 0)
-    col_half = lax.broadcasted_iota(jnp.int32, (half, half), 1)
-    eye_half = row_half == col_half
-    low_half, high_half = pl.ds(0, half), pl.ds(half, half)
-
     def pack(r, w, row):
         last = w[row, 0, high_half, high_half].astype(F32)
         first = jnp.where(col_half >= row_half, w[row, 0, low_half, low_half].astype(F32), last.T)
@@ -361,17 +425,23 @@
     def by_row(js):
         return [[on_copy(j) for j in js if rest[j][0] == r] for r in range(rows)]
 
-    relayed, relayed_edge = by_row(range(n_plain)), by_row(range(n_edge))
-    direct_rest = [[x_rest(from_first, 0, BW - DIRECT, BW)] if r == 0 and DIRECT else [] for r in range(rows)]
-    direct_rest_edge = [
-        [x_rest(from_first, 0, BW - DIRECT_EDGE, BW)] if r == 0 and DIRECT_EDGE else [] for r in range(rows)
-    ]
+    def rest_kind(count):
+        by_link = by_row(range(len(rest) - count))
+        by_link[0].append(x_rest(from_first, 0, BW - count, BW))
+        return by_link
+
+    rest_kinds = (
+        (jnp.logical_and(from_relay, grp > 0), rest_kind(DIRECT)),
+        (edge_in, rest_kind(DIRECT_EDGE)),
+    )
     beside_rest = [[x_rest(from_first, r, 0, BW - r)] for r in range(rows)]
     x_first = [[x_crit(from_first, r, BW + 1)] for r in range(rows)]
     x_first_edge = [[x_crit(from_first, r, BW)] if r else [] for r in range(rows)]
     y_first = [[y_part(w1.at[BW + r], r, 0)] if r else [] for r in range(rows)]
     y_rest = [[y_part(w1.at[BW + r], r, kind) for kind in ((1, 2) if r < rows - 1 else (2,))] for r in range(rows)]
     y_rest[rows - 1].append(corner_copy)
+    y_last, y_rest[0] = y_rest[0], []
+    y_last_edge = y_edge() + [y_part(w1.at[BW], 0, 2)] + [side_on(k) for k in range(1, n_side + 1)]
 
     @pl.when(edge_in)
     def _():
@@ -397,7 +467,10 @@
         def _():
             keep = above[pl.ds(rows + r, 1), :] >= float(BW)
             base[r] = scaled(base[r], r, r + BW, keep)
-            first_diag = scaled_diag(diag0[r], r, above[pl.ds(r, 1), :])
+            first = diag0[r, :, low_half].astype(F32)
+            top = jnp.concatenate([first, jnp.zeros((half, half), F32)], axis=1)
+            bottom = jnp.concatenate([diag0[r, :, high_half].astype(F32), first.T], axis=1)
+            first_diag = scaled_diag(jnp.concatenate([top, bottom], axis=0), r, above[pl.ds(r, 1), :])
             w0[r, BW] = last_column(r, first_diag, base[r])
 
         upper_row(r, w0, l0, w1, BW + r, 0)
@@ -409,7 +482,7 @@
     def _():
         def clear(a, c):
             base[a] = jnp.zeros((size, size), BF16)
-            diag0[a] = jnp.zeros((size, size), BF16)
+            diag0[a] = jnp.zeros((half, size), BF16)
             return c
 
         lax.fori_loop(0, rows, clear, 0)
@@ -427,17 +500,13 @@
             x_crit(from_first, r, BW).start()
         for j in range(n_edge):
             out_copy(j).start()
-        if DIRECT_EDGE:
-            x_rest(from_first, 0, BW - DIRECT_EDGE, BW).start()
+        x_rest(from_first, 0, BW - DIRECT_EDGE, BW).start()
 
     def lower_1(i, c):
         r = rows - 1 - i
         arrive(r, beside_rest, odd)
-        plain = jnp.logical_and(from_relay, grp > 0)
-        arrive(r, relayed, plain)
-        arrive(r, direct_rest, plain)
-        arrive(r, relayed_edge, edge_in)
-        arrive(r, direct_rest_edge, edge_in)
+        for kind, pieces in rest_kinds:
+            arrive(r, pieces, kind)
 
         @pl.when(grp > 0)
         def _():
@@ -462,10 +531,7 @@
         for part in y_parts(lambda r: w1.at[BW + r]):
             part.start()
 
-
-    @pl.when(grp < n_grp - 1)
-    def _():
-        forward(range(half_way, n_most))
+    forward(range(half_way, n_most))
 
     def upper_2(i, c):
         r = rows - 1 - i
@@ -482,6 +548,8 @@
     def lower_2(i, c):
         r = rows - 1 - i
         arrive(r, y_rest, has_prev)
+        arrive(r, [y_last] + [[]] * (rows - 1), grp > 0)
+        arrive(r, [y_last_edge] + [[]] * (rows - 1), edge_in)
 
         @pl.when(has_prev)
         def _():
@@ -491,18 +559,23 @@
         lower_row(r, w1, l1, lo, again)
         return c
 
+    for k in range(1, n_side + 1):
+
+        @pl.when(jnp.logical_and(on_side, side_back == k))
+        def _():
+            side_out(k).wait_recv()
+            side_on(k).start()
+
     @pl.when(odd)
     def _():
         lax.fori_loop(0, rows, upper_2, 0)
 
     @pl.when(edge_out)
     def _():
-        for part in y_parts(lambda r: wo.at[r]):
+        for k in range(1, n_side + 1):
+            side_out(k).start()
+        for part in y_parts_edge():
             part.start()
-
-    @pl.when(grp == n_grp - 1)
-    def _():
-        forward(range(half_way, n_most))
 
     def finish(i, c):
         @pl.when(jnp.logical_not(odd))
@@ -517,11 +590,18 @@
 
     @pl.when(has_next)
     def _():
-        for part in y_parts(lambda r: w1.at[BW + r]) + [to_next]:
+        to_next.wait_send()
+
+    for k in range(1, n_side + 1):
+
+        @pl.when(jnp.logical_and(on_side, side_back == k))
+        def _():
+            side_on(k).wait_send()
+
+    @pl.when(inside)
+    def _():
+        for part in y_parts(lambda r: w1.at[BW + r]):
             part.wait_send()
-
-    @pl.when(inside)
-    def _():
         for r in downward:
             x_crit(from_first, r, BW + 1).wait_send()
 
@@ -538,24 +618,24 @@
 
     @pl.when(edge_out)
     def _():
+        for k in range(1, n_side + 1):
+            side_out(k).wait_send()
+        for part in y_parts_edge():
+            part.wait_send()
         for copy in g_copies:
             copy.wait_send()
         for r in range(rows - 1, 0, -1):
             x_crit(from_first, r, BW).wait_send()
         for j in range(n_edge):
             out_copy(j).wait_send()
-        if DIRECT_EDGE:
-            x_rest(from_first, 0, BW - DIRECT_EDGE, BW).wait_send()
-
-    @pl.when(relaying_plain)
-    def _():
-        for j in range(n_plain):
-            on_copy(j).wait_send()
-
-    @pl.when(origin_edge)
-    def _():
-        for j in range(n_edge):
-            on_copy(j).wait_send()
+        x_rest(from_first, 0, BW - DIRECT_EDGE, BW).wait_send()
+
+    for kind, count in by_kind:
+
+        @pl.when(kind)
+        def _():
+            for j in range(count):
+                on_copy(j).wait_send()
 
     @pl.when(has_prev)
     def _():
@@ -581,7 +661,9 @@
             pltpu.VMEM((2 * rows, BW + 1) + block, BF16),
             pltpu.VMEM((rows, BW) + block, BF16),
             pltpu.VMEM((rows,) + block, BF16),
-            pltpu.VMEM((rows,) + block, BF16),
+            pltpu.VMEM((rows, size // 2, size), BF16),
+            pltpu.VMEM((rows, size // 2, size), BF16),
+            pltpu.VMEM((1,) + block, BF16),
             pltpu.VMEM((n_rest,) + block, BF16),
             pltpu.VMEM((rows, size // 2, size), BF16),
             pltpu.VMEM((2 * rows, size // 2), F32),
@@ -604,7 +686,7 @@
             pltpu.SemaphoreType.DMA((4 * rows,)),
             pltpu.SemaphoreType.DMA((3,)),
             pltpu.SemaphoreType.DMA((3,)),
-        ] + [pltpu.SemaphoreType.DMA((n_rest,))] * 4,
+        ] + [pltpu.SemaphoreType.DMA((n_rest,))] * 4 + [pltpu.SemaphoreType.DMA((rows,))] * 4,
         compiler_params=pltpu.CompilerParams(
             collective_id=0, has_side_effects=True, vmem_limit_bytes=67_043_328 - 2 * blocks.size
         ),

time: 96.9 us -> 93.9 us (0.969)
  Pallas kernels: 94.6 us -> 91.6 us
    pallas_call x1, Pallas kernels: 94.6 us -> 91.6 us  [per_device(): return call(blocks, diag_shift, offsets.T)]
where the time goes in v4:
time: 93.9 us; the launch traced here: 93.8 us
  Pallas kernels  91.6 us (98%)
  local copies, waits for them, and re-layouts  2.19 us (2%)
    pallas_call x1, Pallas kernels, per_device(): return call(blocks, diag_shift, offsets.T)  91.6 us
    unnamed x1, local copies, waits for them, and re-layouts  2.19 us

profile of v4, /device:TPU:38, one launch (start us, length us, event | category | flops | bytes accessed | tf_op | source)
XLA Modules:
  0.0 93.8 jit_solution(3878357567719357776)
XLA Ops:
  0.0 91.6 %sweeps.1 = bf16[4,9,256,256]{3,2,1,0:T(8,128)(2,1)S(1)} custom-call(bf16[4,9,256,256]{3,2,1,0:T(8,128)(2,1)} %blocks.1, f32[1024]{0:T(1024)} %shift_in.1, s32[2,4]{1,0:T(2,128)} %bitcast.1), custom_call_target="tpu_custom_call" | custom-call | tf_op jit(solution)/shard_map/sweeps/pallas_call | solution.py:695
  91.7 2.2 %copy.5 = bf16[4,9,256,256]{3,2,1,0:T(8,128)(2,1)} copy(bf16[4,9,256,256]{3,2,1,0:T(8,128)(2,1)S(1)} %sweeps.1) | data formatting | bytes 9437184

commit v5 on v4

--- a/solution.py
+++ b/solution.py
@@ -14,7 +14,7 @@
 LANES = 128
 DIRECT = 2
 DIRECT_EDGE = 3
-HEAD = 2
+HEAD = 1
 CHIPS_ZH = 4
 
 

time: 93.9 us -> 93.4 us (level)
  Pallas kernels: 91.6 us -> 90.3 us
    pallas_call x1, Pallas kernels: 91.6 us -> 90.3 us  [per_device(): return call(blocks, diag_shift, offsets.T)]
where the time goes in v5:
time: 93.4 us; the launch traced here: 92.5 us
  Pallas kernels  90.3 us (97%)
  local copies, waits for them, and re-layouts  2.19 us (2%)
    pallas_call x1, Pallas kernels, per_device(): return call(blocks, diag_shift, offsets.T)  90.3 us
    unnamed x1, local copies, waits for them, and re-layouts  2.19 us

profile of v5, /device:TPU:38, one launch (start us, length us, event | category | flops | bytes accessed | tf_op | source)
XLA Modules:
  0.0 92.5 jit_solution(6304716775924156411)
XLA Ops:
  0.0 90.3 %sweeps.1 = bf16[4,9,256,256]{3,2,1,0:T(8,128)(2,1)S(1)} custom-call(bf16[4,9,256,256]{3,2,1,0:T(8,128)(2,1)} %blocks.1, f32[1024]{0:T(1024)} %shift_in.1, s32[2,4]{1,0:T(2,128)} %bitcast.1), custom_call_target="tpu_custom_call" | custom-call | tf_op jit(solution)/shard_map/sweeps/pallas_call | solution.py:695
  90.3 2.2 %copy.5 = bf16[4,9,256,256]{3,2,1,0:T(8,128)(2,1)} copy(bf16[4,9,256,256]{3,2,1,0:T(8,128)(2,1)S(1)} %sweeps.1) | data formatting | bytes 9437184
